TPU v7x, 32 devices: a whole 2x2x4 slice. The times are simulated.
32 devices in a mesh: dp: 8 (over z, core), tp: 4 (over y, x).
Axes of the slice: x: 2, y: 2, z: 4, core: 2. Of those that a mesh axis runs over, the one named last changes fastest.
Arguments:
- hidden_states: bfloat16 [2048, 3584], P('dp'), may hold values from -21 to 21
- resp_lengths: int32 [4], replicated, may hold values from 1 to 1280, 2048 in all
- w_query: bfloat16 [3584, 512], P('dp', 'tp'), may hold values from -0.25 to 0.25
- w_keyval: bfloat16 [3584, 1024], P('dp', 'tp'), may hold values from -0.09375 to 0.09375
- w_out: bfloat16 [512, 3584], P('tp', 'dp'), may hold values from -0.25 to 0.25
Outputs:
- attended: bfloat16 [2048, 3584], P('dp', 'tp')
Inputs may be any that keep to these rules, and one draw needn't show every extreme that they name: `resp_lengths`: the 4 lengths sum to 2048; the longest is exactly 1280.
All inputs are finite; a program needn't handle non-finite values.
Results may differ from a plain program's by a relative error of at most 0.015.
The roundings to bfloat16 on the way count: a program that leaves them out, or rounds other values in their place, can miss the bound.
Values may be sent and summed in bfloat16 or wider, within the bound.
No kernel may reach another device: no remote copies, remote signals or barrier semaphores. Data moves between devices by JAX's collectives and lax.ppermute only.
A program may use at most 64 MiB of HBM per device.

v0:
```python
import jax
import jax.numpy as jnp
from jax import lax
from jax.sharding import PartitionSpec as P

HD = 128


def segment_of(position, resp_ends):
    return jnp.sum(
        (position[:, None] >= resp_ends[None, :]).astype(jnp.int32), axis=1, dtype=jnp.int32
    )


def body(hidden_states, resp_lengths, w_query, w_keyval, w_out):
    token_rows = hidden_states.shape[0]
    head_scale = HD ** (-0.5)
    pieces = (
        lax.all_gather(w_query, "dp", axis=0, tiled=True),
        lax.all_gather(w_keyval, "dp", axis=0, tiled=True),
    )
    query_sum = jnp.dot(hidden_states, pieces[0], preferred_element_type=jnp.float32)
    keyval_sum = jnp.dot(hidden_states, pieces[1], preferred_element_type=jnp.float32)
    query = (query_sum * head_scale).astype(jnp.bfloat16)
    keyval = lax.all_gather(keyval_sum.astype(jnp.bfloat16), "tp", axis=1, tiled=True)
    kv_count = keyval.shape[1] // (2 * HD)
    per_group = lax.axis_size("tp") // kv_count
    kv_head = lax.axis_index("tp") // per_group
    key_head = lax.dynamic_slice_in_dim(keyval, kv_head * HD, HD, 1)
    value_head = lax.dynamic_slice_in_dim(keyval, (kv_count + kv_head) * HD, HD, 1)
    head_pair = jnp.concatenate([key_head, value_head], axis=1)
    resp_ends = jnp.cumsum(resp_lengths, dtype=jnp.int32)
    own_begin = lax.axis_index("dp") * token_rows
    query_pos = own_begin + jnp.arange(token_rows, dtype=jnp.int32)
    query_seg = segment_of(query_pos, resp_ends)
    pieces = lax.all_gather(head_pair, "dp", axis=0, tiled=True)
    largest = jnp.full((token_rows,), -1e30, jnp.float32)
    height = pieces.shape[0]
    key_pos = jnp.arange(height, dtype=jnp.int32)
    key_seg = segment_of(key_pos, resp_ends)
    scores = jnp.dot(query, pieces[:, :HD].T, preferred_element_type=jnp.float32)
    allowed = (
        (query_seg[:, None] == key_seg[None, :])
        & (key_pos[None, :] <= query_pos[:, None])
        & (key_pos[None, :] >= 0)
    )
    newest = jnp.maximum(largest, jnp.max(jnp.where(allowed, scores, jnp.float32(-1e30)), axis=1))
    expw = jnp.where(allowed, jnp.exp(scores - newest[:, None]), jnp.float32(0.0))
    denom = jnp.sum(expw, axis=1)
    numer = jnp.dot(expw.astype(jnp.bfloat16), pieces[:, HD:], preferred_element_type=jnp.float32)
    heads_out = (numer / denom[:, None]).astype(jnp.bfloat16)
    terms = jnp.dot(
        heads_out,
        lax.all_gather(w_out, "dp", axis=1, tiled=True),
        preferred_element_type=jnp.float32,
    )
    summed = lax.psum_scatter(terms.astype(jnp.bfloat16), "tp", scatter_dimension=1, tiled=True)
    return summed


def solution(mesh):
    return jax.shard_map(
        body,
        mesh=mesh,
        in_specs=(P("dp", None), P(), P("dp", "tp"), P("dp", "tp"), P("tp", "dp")),
        out_specs=P("dp", "tp"),
        check_vma=False,
    )
```

profile of v0, /device:TPU:0, one launch (start us, length us, event | category | flops | bytes accessed | tf_op | source)
XLA Modules:
  0.0 146.7 jit_solution(7602217867818827257)
XLA Ops:
  6.5 0.0 copy-start
  6.5 0.0 all-gather.3.cloned.1.call-start
  6.5 0.7 all-gather.3.cloned.1.call-update
  7.3 0.0 all-gather.5.cloned.1.call-start
  7.3 0.0 copy-start.3
  7.3 0.0 copy-start.1
  7.3 31.4 %all-gather.3.cloned.1.call-done = bf16[3584,256]{1,0:T(8,128)(2,1)} async-done(((bf16[448,256]{1,0:T(8,128)(2,1)}), bf16[3584,256]{1,0:T(8,128)(2,1)}) %all-gather.3.cloned.1.call-update) | async-done | bytes 1835024 | tf_op jit(solution)/shard_map/all_gather | solution.py:20
  38.7 0.0 copy-done
  38.7 2.1 %convolution_convert_fusion.1 = bf16[256,256]{1,0:T(8,128)(2,1)S(1)} fusion(bf16[256,3584]{1,0:T(8,128)(2,1)S(1)} %copy-done, bf16[3584,256]{1,0:T(8,128)(2,1)} %all-gather.3.cloned.1.call-done), kind=kOutput, calls=%fused_computation.7 | convolution fusion | flops 469827584 | bytes 3801088 | tf_op jit(solution)/shard_map/dot_general | solution.py:23
  40.9 0.0 copy-start.2
  40.9 14.4 %all_gather.17 = bf16[256,1024]{1,0:T(8,128)(2,1)S(1)} all-gather(bf16[256,256]{1,0:T(8,128)(2,1)S(1)} %convolution_convert_fusion.1), channel_id=1, replica_groups=mesh['dp'=8,'tp'=4] {'tp'}, dimensions={1}, use_global_device_ids=true | all-gather | bytes 655360 | tf_op jit(solution)/shard_map/all_gather | solution.py:25
  55.3 0.7 pad_maximum_fusion
  56.0 0.0 all-gather.5.cloned.1.call-update
  56.0 0.0 reduce-scatter.4.cloned.1.call-start
  56.0 0.0 copy-done.3
  56.0 0.2 reduce-window.8
  56.2 0.1 convert_reduce_fusion
  56.3 0.1 convert_reduce_fusion.1
  56.4 0.0 copy-done.1
  56.4 19.8 %all_gather.15 = bf16[3584,128]{1,0:T(8,128)(2,1)} all-gather(bf16[448,128]{1,0:T(8,128)(2,1)S(1)} %copy-done.1), channel_id=1, replica_groups=mesh['dp'=8,'tp'=4] {'dp'}, dimensions={0}, use_global_device_ids=true | all-gather | bytes 1032192 | tf_op jit(solution)/shard_map/all_gather | solution.py:19
  76.2 0.0 copy-done.2
  76.2 16.4 %all_gather.19 = bf16[128,3584]{0,1:T(8,128)(2,1)S(1)} all-gather(bf16[128,448]{0,1:T(8,128)(2,1)S(1)} %copy-done.2), channel_id=1, replica_groups=mesh['dp'=8,'tp'=4] {'dp'}, dimensions={1}, use_global_device_ids=true | all-gather | bytes 1032192 | tf_op jit(solution)/shard_map/all_gather | solution.py:54
  92.6 0.0 all-gather.5.cloned.1.call-done
  92.6 3.8 %select_reduce_fusion = (f32[256]{0:T(256)S(1)}, f32[256,2048]{1,0:T(8,128)}) fusion(s32[256]{0:T(256)S(1)} %iota_add_fusion, s32[2048]{0:T(1024)S(1)} %convert_reduce_fusion, s32[256]{0:T(256)S(1)} %convert_reduce_fusion.1, bf16[2048,256]{1,0:T(8,128)(2,1)} %all-gather.5.cloned.1.call-done, bf16[256,3584]{1,0:T(8,128)(2,1)S(1)} %copy-done, ...), kind=kOutput, calls=%fused_computation.2 | convolution fusion | flops 371785472 | bytes 5385216 | tf_op jit(solution)/shard_map/dot_general | solution.py:41
  96.4 2.3 %fusion.1 = f32[256]{0:T(256)S(1)} fusion(f32[256,2048]{1,0:T(8,128)} %get-tuple-element.8, f32[256]{0:T(256)S(1)} %broadcast_maximum_fusion, s32[256]{0:T(256)S(1)} %iota_add_fusion, s32[2048]{0:T(1024)S(1)} %convert_reduce_fusion, s32[256]{0:T(256)S(1)} %convert_reduce_fusion.1), kind=kLoop, calls=%fused_computation.5 | loop fusion | flops 3145472 | bytes 2109440 | tf_op jit(solution)/shard_map/reduce_sum | solution.py:49
  98.7 4.2 %convolution_convert_fusion = bf16[256,3584]{1,0:T(8,128)(2,1)} fusion(bf16[128,3584]{0,1:T(8,128)(2,1)S(1)} %all_gather.19, f32[256,2048]{1,0:T(8,128)} %get-tuple-element.8, f32[256]{0:T(256)S(1)} %broadcast_maximum_fusion, s32[256]{0:T(256)S(1)} %iota_add_fusion, s32[2048]{0:T(1024)S(1)} %convert_reduce_fusion, s32[256]{0:T(256)S(1)} %convert_reduce_fusion.1, ...), kind=kOutput, calls=%fused_computation | convolution fusion | flops 373227520 | bytes 5386240 | tf_op jit(solution)/shard_map/dot_general | solution.py:52
  102.9 3.8 %copy.6 = bf16[256,3584]{0,1:T(8,128)(2,1)} copy(bf16[256,3584]{1,0:T(8,128)(2,1)} %convolution_convert_fusion) | data formatting | bytes 3670016
  106.8 0.0 reduce-scatter.4.cloned.1.call-update
  106.8 31.4 %reduce-scatter.4.cloned.1.call-done = bf16[896,256]{1,0:T(8,128)(2,1)} async-done(((bf16[3584,256]{1,0:T(8,128)(2,1)}), bf16[896,256]{1,0:T(8,128)(2,1)}) %reduce-scatter.4.cloned.1.call-update) | async-done | bytes 458768
  138.2 2.0 %copy.7 = bf16[256,896]{1,0:T(8,128)(2,1)} copy(bf16[256,896]{0,1:T(8,128)(2,1)} %bitcast.10) | data formatting | bytes 917504
  (3 shorter events, 0.0 us)
Async XLA Ops:
  6.5 32.2 %copy-start = (bf16[256,3584]{1,0:T(8,128)(2,1)S(1)}, bf16[256,3584]{1,0:T(8,128)(2,1)}, u32[]{:S(2)}) copy-start(bf16[256,3584]{1,0:T(8,128)(2,1)} %param.5) | copy-start | bytes 5505028
  6.5 32.2 %all-gather.3.cloned.1.call-start = ((), (), s32[]{:S(2)}) async-start(), calls=%async_computation.1 | async-start | bytes 2064384 | tf_op jit(solution)/shard_map/all_gather | solution.py:20
  7.3 85.4 %all-gather.5.cloned.1.call-start = ((), (), s32[]{:S(2)}) async-start(), calls=%async_computation.2 | async-start | bytes 1179648 | tf_op jit(solution)/shard_map/all_gather | solution.py:36
  7.3 48.7 %copy-start.3 = (s32[4]{0:T(128)S(1)}, s32[4]{0:T(128)}, u32[]{:S(2)}) copy-start(s32[4]{0:T(128)} %param.6) | copy-start | bytes 52
  7.3 49.1 %copy-start.1 = (bf16[448,128]{1,0:T(8,128)(2,1)S(1)}, bf16[448,128]{1,0:T(8,128)(2,1)}, u32[]{:S(2)}) copy-start(bf16[448,128]{1,0:T(8,128)(2,1)} %param.7) | copy-start | bytes 344068
  40.9 35.3 %copy-start.2 = (bf16[128,448]{0,1:T(8,128)(2,1)S(1)}, bf16[128,448]{0,1:T(8,128)(2,1)}, u32[]{:S(2)}) copy-start(bf16[128,448]{0,1:T(8,128)(2,1)} %param.9) | copy-start | bytes 344068
  56.0 82.2 %reduce-scatter.4.cloned.1.call-start = ((), (), s32[]{:S(2)}) async-start(), calls=%async_computation.3 | async-start | bytes 2293760
Sparse Core Ops, SparseCore 0:
  9.0 29.6 all-gather.2
  56.1 23.8 all-gather.4
  106.9 31.2 reduce-scatter.3
where the time goes:
time: 147 us
  waiting for transfers between devices  63.6 us (43%)
  blocking collectives  50.6 us (34%)
  between operations  13.2 us (9%)
  matrix products  10.1 us (7%)
  local copies, waits for them, and re-layouts  5.87 us (4%)
  other arithmetic  3.38 us (2%)
    unnamed x4, waiting for transfers between devices  32.2 us
    all_gather x1, waiting for transfers between devices, body(): lax.all_gather(w_keyval, 'dp', axis=0, tiled=True)  31.4 us
    all_gather x1, blocking collectives, body(): lax.all_gather(w_query, 'dp', axis=0, tiled=True)  19.8 us
    all_gather x1, blocking collectives, body(): lax.all_gather(w_out, 'dp', axis=1, tiled=True)  16.4 us
    all_gather x1, blocking collectives, body(): lax.all_gather(keyval_sum.astype(jnp.bfloat16), 'tp', axis=1, tiled=True)  14.4 us
    unnamed x10, local copies, waits for them, and re-layouts  5.84 us
    dot_general x1, matrix products, body(): jnp.dot(heads_out, lax.all_gather(w_out, 'dp', axis=1, tiled=True), prefe...  4.21 us
    dot_general x1, matrix products, body(): jnp.dot(query, pieces[:, :HD].T, preferred_element_type=jnp.float32)  3.75 us
  transfers between devices with their start and end apart: 3, of which 2 were waited for; matrix products, arithmetic and copies ran while one was open for 0% of the time, Pallas kernels for 0%

commit v1 on v0

--- a/solution.py
+++ b/solution.py
@@ -22,7 +22,7 @@
     query_sum = jnp.dot(hidden_states, pieces[0], preferred_element_type=jnp.float32)
     keyval_sum = jnp.dot(hidden_states, pieces[1], preferred_element_type=jnp.float32)
     query = (query_sum * head_scale).astype(jnp.bfloat16)
-    keyval = lax.all_gather(keyval_sum.astype(jnp.bfloat16), "tp", axis=1, tiled=True)
+    keyval = jnp.concatenate(lax.all_gather(keyval_sum.astype(jnp.bfloat16), "tp"), axis=1)
     kv_count = keyval.shape[1] // (2 * HD)
     per_group = lax.axis_size("tp") // kv_count
     kv_head = lax.axis_index("tp") // per_group

time: 147 us -> 143 us (0.973)
  blocking collectives: 50.6 us -> 44.9 us
    all_gather x1, blocking collectives: 14.4 us -> 10.1 us  [body(): lax.all_gather(keyval_sum.astype(jnp.bfloat16), 'tp')]
where the time goes in v1:
time: 143 us
  waiting for transfers between devices  65 us (45%)
  blocking collectives  44.9 us (31%)
  between operations  13.2 us (9%)
  matrix products  10.4 us (7%)
  local copies, waits for them, and re-layouts  6.06 us (4%)
  other arithmetic  3.37 us (2%)
    unnamed x4, waiting for transfers between devices  33.6 us
    all_gather x1, waiting for transfers between devices, body(): lax.all_gather(w_keyval, 'dp', axis=0, tiled=True)  31.4 us
    all_gather x1, blocking collectives, body(): lax.all_gather(w_query, 'dp', axis=0, tiled=True)  18.8 us
    all_gather x1, blocking collectives, body(): lax.all_gather(w_out, 'dp', axis=1, tiled=True)  15.9 us
    all_gather x1, blocking collectives, body(): lax.all_gather(keyval_sum.astype(jnp.bfloat16), 'tp')  10.1 us
    unnamed x10, local copies, waits for them, and re-layouts  5.84 us
    dot_general x1, matrix products, body(): jnp.dot(heads_out, lax.all_gather(w_out, 'dp', axis=1, tiled=True), prefe...  4.51 us
    dot_general x1, matrix products, body(): jnp.dot(query, pieces[:, :HD].T, preferred_element_type=jnp.float32)  3.78 us
  transfers between devices with their start and end apart: 3, of which 2 were waited for; matrix products, arithmetic and copies ran while one was open for 0% of the time, Pallas kernels for 0%

profile of v1, /device:TPU:0, one launch (start us, length us, event | category | flops | bytes accessed | tf_op | source)
XLA Modules:
  0.0 143.1 jit_solution(15164330954555595961)
XLA Ops:
  6.5 0.0 copy-start
  6.5 0.0 all-gather.4.cloned.1.call-start
  6.5 0.7 all-gather.4.cloned.1.call-update
  7.3 0.0 all-gather.6.cloned.1.call-start
  7.3 31.4 %all-gather.4.cloned.1.call-done = bf16[3584,256]{1,0:T(8,128)(2,1)} async-done(((bf16[448,256]{1,0:T(8,128)(2,1)}), bf16[3584,256]{1,0:T(8,128)(2,1)}) %all-gather.4.cloned.1.call-update) | async-done | bytes 1835024 | tf_op jit(solution)/shard_map/all_gather | solution.py:20
  38.7 0.0 copy-done
  38.7 2.1 %convolution_convert_fusion.1 = bf16[256,256]{1,0:T(8,128)(2,1)S(1)} fusion(bf16[256,3584]{1,0:T(8,128)(2,1)S(1)} %copy-done, bf16[3584,256]{1,0:T(8,128)(2,1)} %all-gather.4.cloned.1.call-done), kind=kOutput, calls=%fused_computation.7 | convolution fusion | flops 469827584 | bytes 3801088 | tf_op jit(solution)/shard_map/dot_general | solution.py:23
  40.9 0.0 copy-start.3
  40.9 0.0 copy-start.1
  40.9 0.0 copy-start.2
  40.9 10.1 %all-gather = bf16[1024,256]{1,0:T(8,128)(2,1)S(1)} all-gather(bf16[256,256]{1,0:T(8,128)(2,1)S(1)} %convolution_convert_fusion.1), channel_id=2, replica_groups=mesh['dp'=8,'tp'=4] {'tp'}, dimensions={0}, use_global_device_ids=true | all-gather | bytes 655360 | tf_op jit(solution)/shard_map/all_gather | solution.py:25
  51.0 0.2 copy.8
  51.3 0.7 pad_maximum_fusion
  51.9 0.0 all-gather.6.cloned.1.call-update
  51.9 0.0 reduce-scatter.4.cloned.1.call-start
  52.0 0.0 copy-done.3
  52.0 0.2 reduce-window.8
  52.2 0.1 convert_reduce_fusion
  52.3 0.1 convert_reduce_fusion.1
  52.4 0.0 copy-done.1
  52.4 18.8 %all_gather.18 = bf16[3584,128]{1,0:T(8,128)(2,1)} all-gather(bf16[448,128]{1,0:T(8,128)(2,1)S(1)} %copy-done.1), channel_id=1, replica_groups=mesh['dp'=8,'tp'=4] {'dp'}, dimensions={0}, use_global_device_ids=true | all-gather | bytes 1032192 | tf_op jit(solution)/shard_map/all_gather | solution.py:19
  71.2 0.0 copy-done.2
  71.2 15.9 %all_gather.23 = bf16[128,3584]{0,1:T(8,128)(2,1)S(1)} all-gather(bf16[128,448]{0,1:T(8,128)(2,1)S(1)} %copy-done.2), channel_id=1, replica_groups=mesh['dp'=8,'tp'=4] {'dp'}, dimensions={1}, use_global_device_ids=true | all-gather | bytes 1032192 | tf_op jit(solution)/shard_map/all_gather | solution.py:54
  87.2 0.0 all-gather.6.cloned.1.call-done
  87.2 3.8 %select_reduce_fusion = (f32[256]{0:T(256)S(1)}, f32[256,2048]{1,0:T(8,128)}) fusion(s32[256]{0:T(256)S(1)} %iota_add_fusion, s32[2048]{0:T(1024)S(1)} %convert_reduce_fusion, s32[256]{0:T(256)S(1)} %convert_reduce_fusion.1, bf16[2048,256]{0,1:T(8,128)(2,1)} %all-gather.6.cloned.1.call-done, bf16[256,3584]{1,0:T(8,128)(2,1)S(1)} %copy-done, ...), kind=kOutput, calls=%fused_computation.2 | convolution fusion | flops 371785472 | bytes 5385216 | tf_op jit(solution)/shard_map/dot_general | solution.py:41
  90.9 2.3 %fusion.1 = f32[256]{0:T(256)S(1)} fusion(f32[256,2048]{1,0:T(8,128)} %get-tuple-element.8, f32[256]{0:T(256)S(1)} %broadcast_maximum_fusion, s32[256]{0:T(256)S(1)} %iota_add_fusion, s32[2048]{0:T(1024)S(1)} %convert_reduce_fusion, s32[256]{0:T(256)S(1)} %convert_reduce_fusion.1), kind=kLoop, calls=%fused_computation.5 | loop fusion | flops 3145472 | bytes 2109440 | tf_op jit(solution)/shard_map/reduce_sum | solution.py:49
  93.3 4.5 %convolution_convert_fusion = bf16[256,3584]{1,0:T(8,128)(2,1)} fusion(bf16[128,3584]{0,1:T(8,128)(2,1)S(1)} %all_gather.23, f32[256,2048]{1,0:T(8,128)} %get-tuple-element.8, f32[256]{0:T(256)S(1)} %broadcast_maximum_fusion, s32[256]{0:T(256)S(1)} %iota_add_fusion, s32[2048]{0:T(1024)S(1)} %convert_reduce_fusion, s32[256]{0:T(256)S(1)} %convert_reduce_fusion.1, ...), kind=kOutput, calls=%fused_computation | convolution fusion | flops 373227520 | bytes 5386240 | tf_op jit(solution)/shard_map/dot_general | solution.py:52
  97.8 3.8 %copy.9 = bf16[256,3584]{0,1:T(8,128)(2,1)} copy(bf16[256,3584]{1,0:T(8,128)(2,1)} %convolution_convert_fusion) | data formatting | bytes 3670016
  101.6 0.0 reduce-scatter.4.cloned.1.call-update
  101.6 32.9 %reduce-scatter.4.cloned.1.call-done = bf16[896,256]{1,0:T(8,128)(2,1)} async-done(((bf16[3584,256]{1,0:T(8,128)(2,1)}), bf16[896,256]{1,0:T(8,128)(2,1)}) %reduce-scatter.4.cloned.1.call-update) | async-done | bytes 458768
  134.5 2.0 %copy.10 = bf16[256,896]{1,0:T(8,128)(2,1)} copy(bf16[256,896]{0,1:T(8,128)(2,1)} %bitcast.16) | data formatting | bytes 917504
  (3 shorter events, 0.0 us)
Async XLA Ops:
  6.5 32.2 %copy-start = (bf16[256,3584]{1,0:T(8,128)(2,1)S(1)}, bf16[256,3584]{1,0:T(8,128)(2,1)}, u32[]{:S(2)}) copy-start(bf16[256,3584]{1,0:T(8,128)(2,1)} %param.5) | copy-start | bytes 5505028
  6.5 32.2 %all-gather.4.cloned.1.call-start = ((), (), s32[]{:S(2)}) async-start(), calls=%async_computation.1 | async-start | bytes 2064384 | tf_op jit(solution)/shard_map/all_gather | solution.py:20
  7.3 79.9 %all-gather.6.cloned.1.call-start = ((), (), s32[]{:S(2)}) async-start(), calls=%async_computation.2 | async-start | bytes 1179648 | tf_op jit(solution)/shard_map/all_gather | solution.py:36
  40.9 11.1 %copy-start.3 = (s32[4]{0:T(128)S(1)}, s32[4]{0:T(128)}, u32[]{:S(2)}) copy-start(s32[4]{0:T(128)} %param.6) | copy-start | bytes 52
  40.9 11.5 %copy-start.1 = (bf16[448,128]{1,0:T(8,128)(2,1)S(1)}, bf16[448,128]{1,0:T(8,128)(2,1)}, u32[]{:S(2)}) copy-start(bf16[448,128]{1,0:T(8,128)(2,1)} %param.7) | copy-start | bytes 344068
  40.9 30.4 %copy-start.2 = (bf16[128,448]{0,1:T(8,128)(2,1)S(1)}, bf16[128,448]{0,1:T(8,128)(2,1)}, u32[]{:S(2)}) copy-start(bf16[128,448]{0,1:T(8,128)(2,1)} %param.9) | copy-start | bytes 344068
  51.9 82.6 %reduce-scatter.4.cloned.1.call-start = ((), (), s32[]{:S(2)}) async-start(), calls=%async_computation.3 | async-start | bytes 2293760
Sparse Core Ops, SparseCore 0:
  9.0 29.6 all-gather.3
  52.1 24.8 all-gather.5
  101.8 32.7 reduce-scatter.3
